TPU v7x, 128 devices: a whole 4x4x4 slice. The times are simulated.
128 devices in a mesh: rows: 8 (over z, y_hi), snaps: 16 (over x, y_lo, core).
Axes of the slice: x: 4, y: 4 (y_hi: 2, y_lo: 2; y = y_hi * 2 + y_lo), z: 4, core: 2. Of those that a mesh axis runs over, the one named last changes fastest.
Arguments:
- snapshots: float32 [16384, 4096], P('rows', 'snaps'), may hold values from -6 to 6
- weights: float32 [16384], P('rows'), may hold values from 0.3 to 3
- next_bricks: float32 [16384, 4096], P(('rows', 'snaps')), may hold values from -6 to 6
- brick_source: int32 [8, 64], P('rows'), may hold values from 0 to 63, each once within a row
Outputs:
- gram: float32 [4096, 4096], P('rows', 'snaps')
- next_tiles: float32 [16384, 4096], P('rows', 'snaps')
Inputs may be any that keep to these rules, and one draw needn't show every extreme that they name: Each row of brick_source is a permutation of 0 to 63.
All inputs are finite; a program needn't handle non-finite values.
Results may differ from a plain program's by a relative error of at most 0.00007.
Values sent between devices are 32-bit elements; how exact they have to be, the bound alone decides.
No kernel may reach another device: no remote copies, remote signals or barrier semaphores. Data moves between devices by JAX's collectives and lax.ppermute only.
A program may use at most 128 MiB of HBM per device.

v0:
```python
import math
import jax
import jax.numpy as jnp
from jax import lax
from jax.sharding import Mesh
from jax.sharding import PartitionSpec as P

BRICK = 32
ROWS = ("rows_0", "rows_1")
ROWS_SNAPS = ("rows_0", "rows_1", "snaps")


def scatter_axes(x, axes, dim):
    if not axes:
        return x
    nearer = lax.psum_scatter(x, axes[0], scatter_dimension=dim, tiled=True)
    return scatter_axes(nearer, axes[1:], dim)


def pair_tile(left, right):
    return lax.dot_general(
        left,
        right,
        (((0,), (0,)), ((), ())),
        precision=lax.Precision.HIGHEST,
        preferred_element_type=jnp.float32,
    )


def per_device(snapshots, weights, next_bricks, brick_source):
    width = snapshots.shape[1]
    rows_here = snapshots.shape[0]
    weighted = snapshots * weights[:, None]
    scale = jnp.float32(math.sqrt(rows_here * lax.axis_size(ROWS)))
    column = pair_tile(lax.all_gather(snapshots, "snaps", axis=1, tiled=True), weighted)
    arrived = lax.all_to_all(next_bricks, "snaps", split_axis=1, concat_axis=0, tiled=True)
    bricks = arrived.reshape(-1, BRICK, width)
    next_tiles = jnp.take(bricks, brick_source[0], axis=0).reshape(-1, width)
    summed = scatter_axes(column, ROWS, 0)
    return (summed / scale, next_tiles)


def solution(mesh):
    torus = Mesh(mesh.devices.reshape(4, 2, mesh.shape["snaps"]), ("rows_0", "rows_1", "snaps"))
    in_specs = (P(ROWS, "snaps"), P(ROWS), P(ROWS_SNAPS, None), P(ROWS, None))
    out_specs = (P(ROWS, "snaps"), P(ROWS, "snaps"))
    return jax.shard_map(
        per_device, mesh=torus, in_specs=in_specs, out_specs=out_specs, check_vma=False
    )
```

profile of v0, /device:TPU:1, one launch (start us, length us, event | category | flops | bytes accessed | tf_op | source)
XLA Modules:
  0.0 300.5 jit_solution(7561188030469283432)
XLA Ops:
  7.2 0.0 copy-start
  7.2 0.0 all-gather.2.cloned.1.call-start
  7.2 0.7 all-gather.2.cloned.1.call-update
  7.9 0.0 reduce-scatter.3.cloned.1.call-start
  8.0 175.9 %all-gather.2.cloned.1.call-done = f32[2048,4096]{1,0:T(8,128)} async-done(((f32[2048,256]{1,0:T(8,128)}), f32[2048,4096]{1,0:T(8,128)}) %all-gather.2.cloned.1.call-update) | async-done | bytes 33554448 | tf_op jit(solution)/shard_map/all_gather | solution.py:35
  183.8 0.0 copy-done
  183.8 34.3 %convolution_bitcast_fusion = f32[4096,256]{0,1:T(8,128)} fusion(f32[2048,4096]{1,0:T(8,128)} %all-gather.2.cloned.1.call-done, f32[2048,256]{1,0:T(8,128)S(1)} %copy-done, f32[2048]{0:T(1024)} %param.5), kind=kOutput, calls=%fused_computation.1 | convolution fusion | flops 25770328064 | bytes 39854080 | tf_op jit(solution)/shard_map/dot_general | solution.py:21
  218.2 0.0 copy-start.1
  218.2 0.0 reduce-scatter.3.cloned.1.call-update
  218.2 1.6 copy-done.1
  219.7 1.8 copy.8
  221.5 0.0 copy-start.2
  221.6 5.3 %all-to-all-start = ((f32[128,16,256]{0,2,1:T(8,128)}), f32[128,16,256]{0,2,1:T(8,128)S(1)}, u32[]{:S(2)}, u32[]{:S(2)}) async-start(f32[128,16,256]{0,2,1:T(8,128)} %bitcast.15), calls=%async_computation.2 | async-start | bytes 4194304 | tf_op jit(solution)/shard_map/all_to_all | solution.py:36
  226.8 0.0 reduce-scatter.5.cloned.1.call-start
  226.9 38.7 %reduce-scatter.3.cloned.1.call-done = f32[1024,256]{0,1:T(8,128)} async-done(((f32[4096,256]{0,1:T(8,128)}), f32[1024,256]{0,1:T(8,128)}) %reduce-scatter.3.cloned.1.call-update) | async-done | bytes 1048592 | tf_op jit(solution)/shard_map/reduce_scatter | solution.py:16
  265.6 0.0 reduce-scatter.5.cloned.1.call-update
  265.6 0.0 copy-done.2
  265.6 0.1 broadcast_in_dim.15
  265.7 0.1 broadcast_in_dim.16
  265.8 0.0 all-to-all-done
  265.8 1.8 copy.9
  267.7 2.3 gather_fusion
  269.9 1.7 bitcast_select_fusion
  271.6 20.3 %reduce-scatter.5.cloned.1.call-done = f32[512,256]{0,1:T(8,128)} async-done(((f32[1024,256]{0,1:T(8,128)}), f32[512,256]{0,1:T(8,128)}) %reduce-scatter.5.cloned.1.call-update) | async-done | bytes 524304 | tf_op jit(solution)/shard_map/reduce_scatter | solution.py:16
  291.9 1.1 broadcast_multiply_fusion
  293.0 1.0 copy.10
  (3 shorter events, 0.0 us)
Async XLA Ops:
  7.2 176.7 %copy-start = (f32[2048,256]{1,0:T(8,128)S(1)}, f32[2048,256]{1,0:T(8,128)}, u32[]{:S(2)}) copy-start(f32[2048,256]{1,0:T(8,128)} %param.4) | copy-start | bytes 6291460
  7.2 176.7 %all-gather.2.cloned.1.call-start = ((), (), s32[]{:S(2)}) async-start(), calls=%async_computation.3 | async-start | bytes 35651584 | tf_op jit(solution)/shard_map/all_gather | solution.py:35
  7.9 257.7 %reduce-scatter.3.cloned.1.call-start = ((), (), s32[]{:S(2)}) async-start(), calls=%async_computation.4 | async-start | bytes 5242880 | tf_op jit(solution)/shard_map/reduce_scatter | solution.py:16
  218.2 1.6 copy-start.1
  221.5 44.1 %copy-start.2 = (s32[1,64]{1,0:T(1,128)S(1)}, s32[1,64]{1,0:T(1,128)}, u32[]{:S(2)}) copy-start(s32[1,64]{1,0:T(1,128)} %param.7) | copy-start | bytes 772
  221.6 44.3 %all-to-all-start = ((f32[128,16,256]{0,2,1:T(8,128)}), f32[128,16,256]{0,2,1:T(8,128)S(1)}, u32[]{:S(2)}, u32[]{:S(2)}) async-start(f32[128,16,256]{0,2,1:T(8,128)} %bitcast.15), calls=%async_computation.2 | async-start | bytes 4194304 | tf_op jit(solution)/shard_map/all_to_all | solution.py:36
  226.8 65.1 %reduce-scatter.5.cloned.1.call-start = ((), (), s32[]{:S(2)}) async-start(), calls=%async_computation.5 | async-start | bytes 1572864 | tf_op jit(solution)/shard_map/reduce_scatter | solution.py:16
Sparse Core Ops, SparseCore 0:
  9.6 174.1 all-gather.1
  218.3 47.2 reduce-scatter.2
  268.0 23.8 reduce-scatter.4
where the time goes:
time: 301 us
  waiting for transfers between devices  236 us (78%)
  matrix products  34.3 us (11%)
  between operations  13.8 us (5%)
  local copies, waits for them, and re-layouts  8.62 us (3%)
  starting transfers between devices  5.38 us (2%)
    all_gather x1, waiting for transfers between devices, per_device(): lax.all_gather(snapshots, 'snaps', axis=1, tiled=True)  176 us
    reduce_scatter x2, waiting for transfers between devices, scatter_axes(): nearer = lax.psum_scatter(x, axes[0], scatter_dimension=dim, tiled=True)  59 us
    dot_general x1, matrix products, pair_tile(): lax.dot_general(left, right, (((0,), (0,)), ((), ())), precision=lax.Prec...  34.3 us
  transfers between devices with their start and end apart: 4, of which 3 were waited for; matrix products, arithmetic and copies ran while one was open for 3% of the time, Pallas kernels for 0%

commit v1 on v0

--- a/solution.py
+++ b/solution.py
@@ -32,7 +32,12 @@
     rows_here = snapshots.shape[0]
     weighted = snapshots * weights[:, None]
     scale = jnp.float32(math.sqrt(rows_here * lax.axis_size(ROWS)))
-    column = pair_tile(lax.all_gather(snapshots, "snaps", axis=1, tiled=True), weighted)
+    column = pair_tile(
+        jnp.concatenate(
+            lax.all_to_all(jnp.stack([snapshots] * lax.axis_size("snaps")), "snaps", 0, 0), axis=1
+        ),
+        weighted,
+    )
     arrived = lax.all_to_all(next_bricks, "snaps", split_axis=1, concat_axis=0, tiled=True)
     bricks = arrived.reshape(-1, BRICK, width)
     next_tiles = jnp.take(bricks, brick_source[0], axis=0).reshape(-1, width)

time: 301 us -> 531 us (1.76)
  blocking collectives: 0 us -> 372 us
  waiting for transfers between devices: 236 us -> 60.2 us
  matrix products: 34.3 us -> 59.7 us
  local copies, waits for them, and re-layouts: 8.62 us -> 14.7 us
    all_to_all x0 -> x1, blocking collectives: none -> 372 us  [per_device(): lax.all_to_all(jnp.stack([snapshots] * lax.axis_size('snaps')), 'snaps',...]
    all_gather x1 -> x0, waiting for transfers between devices: 176 us -> none  [per_device(): lax.all_gather(snapshots, 'snaps', axis=1, tiled=True)]
    dot_general x1, matrix products: 34.3 us -> 59.7 us  [pair_tile(): lax.dot_general(left, right, (((0,), (0,)), ((), ())), precision=lax.Prec...]
  transfers between devices with their start and end apart: 4 -> 3, of which waited for: 3 -> 2; matrix products, arithmetic and copies ran while one was open for 3% -> 1% of each run, Pallas kernels for 0% -> 0%
where the time goes in v1:
time: 531 us
  blocking collectives  372 us (70%)
  waiting for transfers between devices  60.2 us (11%)
  matrix products  59.7 us (11%)
  local copies, waits for them, and re-layouts  14.7 us (3%)
  between operations  14.1 us (3%)
  starting transfers between devices  6.88 us (1%)
    all_to_all x1, blocking collectives, per_device(): lax.all_to_all(jnp.stack([snapshots] * lax.axis_size('snaps')), 'snaps',...  372 us
    reduce_scatter x2, waiting for transfers between devices, scatter_axes(): nearer = lax.psum_scatter(x, axes[0], scatter_dimension=dim, tiled=True)  60.1 us
    dot_general x1, matrix products, pair_tile(): lax.dot_general(left, right, (((0,), (0,)), ((), ())), precision=lax.Prec...  59.7 us
  transfers between devices with their start and end apart: 3, of which 2 were waited for; matrix products, arithmetic and copies ran while one was open for 1% of the time, Pallas kernels for 0%

profile of v1, /device:TPU:1, one launch (start us, length us, event | category | flops | bytes accessed | tf_op | source)
XLA Modules:
  0.0 530.5 jit_solution(1128492779243163851)
XLA Ops:
  7.2 0.0 reduce-scatter.3.cloned.1.call-start
  7.2 1.9 copy.9
  9.1 4.1 stack.2
  13.3 0.0 copy-start
  13.3 0.0 copy-start.2
  13.3 372.2 %all_to_all.21 = f32[16,2048,256]{1,2,0:T(8,128)} all-to-all(f32[16,2048,256]{1,2,0:T(8,128)S(1)} %stack.2), channel_id=1, replica_groups=mesh['rows_0'=4,'rows_1'=2,'snaps'=16] {'snaps'}, dimensions={0} | all-to-all | bytes 67108864 | tf_op jit(solution)/shard_map/all_to_all | solution.py:37
  385.6 0.0 copy-done
  385.6 0.0 copy-done.2
  385.6 59.7 %convolution_bitcast_fusion = f32[4096,256]{0,1:T(8,128)} fusion(f32[2048,4096]{0,1:T(8,128)} %bitcast.17, f32[2048,256]{1,0:T(8,128)S(1)} %copy-done, f32[2048]{0:T(1024)S(1)} %copy-done.2), kind=kOutput, calls=%fused_computation.1 | convolution fusion | flops 25770328064 | bytes 39854080 | tf_op jit(solution)/shard_map/dot_general | solution.py:21
  445.2 0.0 copy-start.1
  445.2 0.0 reduce-scatter.3.cloned.1.call-update
  445.3 1.6 copy-done.1
  446.8 1.8 copy.10
  448.6 0.0 copy-start.3
  448.6 6.8 %all-to-all-start.1 = ((f32[128,16,256]{0,2,1:T(8,128)}), f32[128,16,256]{0,2,1:T(8,128)S(1)}, u32[]{:S(2)}, u32[]{:S(2)}) async-start(f32[128,16,256]{0,2,1:T(8,128)} %bitcast.19), calls=%async_computation.3 | async-start | bytes 4194304 | tf_op jit(solution)/shard_map/all_to_all | solution.py:41
  455.4 0.0 reduce-scatter.5.cloned.1.call-start
  455.5 39.8 %reduce-scatter.3.cloned.1.call-done = f32[1024,256]{0,1:T(8,128)} async-done(((f32[4096,256]{0,1:T(8,128)}), f32[1024,256]{0,1:T(8,128)}) %reduce-scatter.3.cloned.1.call-update) | async-done | bytes 1048592 | tf_op jit(solution)/shard_map/reduce_scatter | solution.py:16
  495.3 0.0 reduce-scatter.5.cloned.1.call-update
  495.3 0.0 copy-done.3
  495.3 0.1 broadcast_in_dim.15
  495.4 0.1 broadcast_in_dim.16
  495.5 0.0 all-to-all-done.1
  495.5 1.8 copy.11
  497.3 2.3 gather_fusion
  499.6 1.7 bitcast_select_fusion
  501.3 20.3 %reduce-scatter.5.cloned.1.call-done = f32[512,256]{0,1:T(8,128)} async-done(((f32[1024,256]{0,1:T(8,128)}), f32[512,256]{0,1:T(8,128)}) %reduce-scatter.5.cloned.1.call-update) | async-done | bytes 524304 | tf_op jit(solution)/shard_map/reduce_scatter | solution.py:16
  521.6 1.1 broadcast_multiply_fusion
  522.7 1.0 copy.12
  (3 shorter events, 0.0 us)
Async XLA Ops:
  7.2 488.1 %reduce-scatter.3.cloned.1.call-start = ((), (), s32[]{:S(2)}) async-start(), calls=%async_computation.4 | async-start | bytes 5242880 | tf_op jit(solution)/shard_map/reduce_scatter | solution.py:16
  13.3 372.3 %copy-start = (f32[2048,256]{1,0:T(8,128)S(1)}, f32[2048,256]{1,0:T(8,128)}, u32[]{:S(2)}) copy-start(f32[2048,256]{1,0:T(8,128)} %param.4) | copy-start | bytes 6291460
  13.3 372.3 %copy-start.2 = (f32[2048]{0:T(1024)S(1)}, f32[2048]{0:T(1024)}, u32[]{:S(2)}) copy-start(f32[2048]{0:T(1024)} %param.5) | copy-start | bytes 24580
  445.2 1.6 copy-start.1
  448.6 46.7 %copy-start.3 = (s32[1,64]{1,0:T(1,128)S(1)}, s32[1,64]{1,0:T(1,128)}, u32[]{:S(2)}) copy-start(s32[1,64]{1,0:T(1,128)} %param.7) | copy-start | bytes 772
  448.6 46.9 %all-to-all-start.1 = ((f32[128,16,256]{0,2,1:T(8,128)}), f32[128,16,256]{0,2,1:T(8,128)S(1)}, u32[]{:S(2)}, u32[]{:S(2)}) async-start(f32[128,16,256]{0,2,1:T(8,128)} %bitcast.19), calls=%async_computation.3 | async-start | bytes 4194304 | tf_op jit(solution)/shard_map/all_to_all | solution.py:41
  455.4 66.2 %reduce-scatter.5.cloned.1.call-start = ((), (), s32[]{:S(2)}) async-start(), calls=%async_computation.5 | async-start | bytes 1572864 | tf_op jit(solution)/shard_map/reduce_scatter | solution.py:16
Sparse Core Ops, SparseCore 0:
  445.4 49.8 reduce-scatter.2
  497.6 23.9 reduce-scatter.4
